TPU v7x, 256 devices: a whole 4x4x8 slice. The times are simulated.
256 devices in a mesh: seq: 32 (over y, z), head: 8 (over x, core).
Axes of the slice: x: 4, y: 4, z: 8, core: 2. Of those that a mesh axis runs over, the one named last changes fastest.
Arguments:
- tokens: bfloat16 [32768, 2048], P(('seq', 'head')), may hold values from -6 to 6
- w_in_x: bfloat16 [2048, 4096], P(None, 'head'), may hold values from -0.125 to 0.125
- w_in_z: bfloat16 [2048, 4096], P(None, 'head'), may hold values from -0.125 to 0.125
- w_in_bc: bfloat16 [2048, 256], replicated, may hold values from -0.125 to 0.125
- w_dt: bfloat16 [2048, 64], P(None, 'head'), may hold values from -0.125 to 0.125
- conv_x: float32 [4, 4096], P(None, 'head'), may hold values from -3 to 3
- conv_bc: float32 [4, 256], replicated, may hold values from -3 to 3
- dt_bias: float32 [64], P('head'), may hold values from -1 to 1
- decay_rate: float32 [64], P('head'), may hold values from 1.5258789e-06 to 0.05, as said below
- skip: float32 [64], P('head'), may hold values from 0.5 to 1.5
- norm_gain: float32 [4096], P('head'), may hold values from 0.25 to 1.75
- w_out: bfloat16 [4096, 2048], P('head'), may hold values from -0.09375 to 0.09375
Outputs:
- mixed: bfloat16 [32768, 2048], P(('seq', 'head'))
Inputs may be any that keep to these rules, and one draw needn't show every extreme that they name: `decay_rate`: positive per-head decay rates.
All inputs are finite; a program needn't handle non-finite values.
Results may differ from a plain program's by a relative error of at most 0.013.
Values may be sent and summed in bfloat16 or wider, within the bound.
No kernel may reach another device: no remote copies, remote signals or barrier semaphores. Data moves between devices by JAX's collectives and lax.ppermute only.
A program may use at most 128 MiB of HBM per device.

v0:
```python
import jax
import jax.numpy as jnp
from jax import lax
from jax.sharding import Mesh
from jax.sharding import PartitionSpec as P

SPAN = 256
KERNEL = 4
E = 4096
SEQ = ("seq_0", "seq_1")
SEQ_HEAD = ("seq_0", "seq_1", "head")
highest = lax.Precision.HIGHEST


def passed_along(block, axis, distance):
    devices = range(lax.axis_size(axis))
    route = [(i - distance, i) for i in devices if i - distance in devices]
    return lax.ppermute(block, axis, route)


def neutral_like(shard, identity):
    return jax.tree.map(
        lambda part, zero: jnp.zeros_like(part) + jnp.asarray(zero, part.dtype), shard, identity
    )


def entering_2(shard, axes, combine, identity):
    before = start = neutral_like(shard, identity)
    running = shard
    for axis in reversed(axes):
        size, index = (lax.axis_size(axis), lax.axis_index(axis))
        pieces = jax.tree.map(lambda part: lax.all_gather(part, axis), running)
        inside, running = (start, start)
        for k in range(size):
            passed = k < index
            running = combine(running, jax.tree.map(lambda part: part[k], pieces))
            inside = jax.tree.map(lambda new, old: jnp.where(passed, new, old), running, inside)
        before = combine(inside, before)
    return before


def sent_to_all(shard, axis):
    size = lax.axis_size(axis)
    return lax.all_to_all(
        jnp.broadcast_to(shard[None], (size, *shard.shape)), axis, 0, 0, tiled=True
    )


def over_copies(shard, axis):
    everything = sent_to_all(shard, axis)
    return jnp.sum(everything, axis=0)


def span_update(state, x_span, step_span, decay_span, b_span, c_span, skip):
    cumul = jnp.cumsum(decay_span, axis=0)
    length = x_span.shape[0]
    lower = jnp.arange(length)[:, None] >= jnp.arange(length)[None, :]
    spread = cumul.T[:, :, None] - cumul.T[:, None, :]
    within = jnp.exp(jnp.where(lower[None], spread, -jnp.inf))
    scores = jnp.dot(c_span, b_span.T, precision=highest)
    scaled = x_span * step_span[:, :, None]
    output = jnp.einsum("hts,shp->thp", within * scores[None], scaled, precision=highest)
    output = (
        output
        + jnp.einsum("tn,hpn->thp", c_span, state, precision=highest) * jnp.exp(cumul)[:, :, None]
    )
    output = output + skip[None, :, None] * x_span
    remain = jnp.exp(cumul[-1][None, :] - cumul)
    fresh = jnp.einsum("shp,sn->hpn", scaled * remain[:, :, None], b_span, precision=highest)
    return (jnp.exp(cumul[-1])[:, None, None] * state + fresh, output, cumul)


def causal_conv(values, before, kernel):
    padded = jnp.concatenate([before, values], axis=0)
    length = values.shape[0]
    result = kernel[0] * padded[0:length]
    for offset in range(1, kernel.shape[0]):
        result = result + kernel[offset] * padded[offset : offset + length]
    return jax.nn.silu(result)


def per_device(
    tokens,
    w_in_x,
    w_in_z,
    w_in_bc,
    w_dt,
    conv_x,
    conv_bc,
    dt_bias,
    decay_rate,
    skip,
    norm_gain,
    w_out,
):
    inner_cols = w_in_x.shape[1]
    head_count = dt_bias.shape[0]
    head_width = inner_cols // head_count
    state_size = w_in_bc.shape[1] // 2
    block_rows = lax.all_gather(tokens, "head", axis=0, tiled=True)
    joined = jnp.concatenate(
        [
            jnp.dot(block_rows, w_in_x, preferred_element_type=jnp.float32),
            jnp.dot(block_rows, w_in_z, preferred_element_type=jnp.float32),
            jnp.dot(block_rows, w_in_bc, preferred_element_type=jnp.float32),
            jnp.dot(block_rows, w_dt, preferred_element_type=jnp.float32),
        ],
        axis=1,
    )
    x_proj = joined[:, :inner_cols]
    gate_proj = joined[:, inner_cols : 2 * inner_cols]
    bc_proj = joined[:, 2 * inner_cols : 2 * inner_cols + 2 * state_size]
    step_raw = joined[:, 2 * inner_cols + 2 * state_size :]
    margin = KERNEL - 1
    x_before, bc_before = passed_along((x_proj[-margin:], bc_proj[-margin:]), SEQ, 1)
    x_conv = causal_conv(x_proj, x_before, conv_x)
    bc_conv = causal_conv(bc_proj, bc_before, conv_bc)
    step_size = jax.nn.softplus(step_raw + dt_bias)
    log_decay = -step_size * decay_rate
    seg_rows = x_proj.shape[0]
    spans = seg_rows // SPAN

    def advance(carry, inputs):
        state, offset = carry
        x_span, step_span, decay_span, bc_span = inputs
        state, output, cumul = span_update(
            state,
            x_span,
            step_span,
            decay_span,
            bc_span[:, :state_size],
            bc_span[:, state_size:],
            skip,
        )
        return ((state, offset + cumul[-1]), (output, cumul + offset))

    empty_state = jnp.zeros((head_count, head_width, state_size), jnp.float32)
    empty_decay = jnp.zeros((head_count,), jnp.float32)
    (final_state, totals), (outputs, cumuls) = lax.scan(
        advance,
        (empty_state, empty_decay),
        (
            x_conv.reshape(spans, SPAN, head_count, head_width),
            step_size.reshape(spans, SPAN, head_count),
            log_decay.reshape(spans, SPAN, head_count),
            bc_conv.reshape(spans, SPAN, 2 * state_size),
        ),
    )
    local_out = outputs.reshape(seg_rows, head_count, head_width)
    segment_cumul = cumuls.reshape(seg_rows, head_count)

    def combine(earlier, later):
        return (earlier[0] + later[0], jnp.exp(later[0])[:, None, None] * earlier[1] + later[1])

    entering = entering_2((totals, final_state), SEQ, combine, (empty_decay, empty_state))[1]
    c_matrix = bc_conv[:, state_size:]
    carried = (
        jnp.einsum("tn,hpn->thp", c_matrix, entering, precision=highest)
        * jnp.exp(segment_cumul)[:, :, None]
    )
    ssd_out = (local_out + carried).reshape(seg_rows, inner_cols)
    gated = ssd_out * jax.nn.silu(gate_proj)
    squares = over_copies(jnp.sum(gated * gated, axis=1), "head")
    normed = (gated * lax.rsqrt(squares / E + 1e-05)[:, None] * norm_gain).astype(jnp.bfloat16)
    result = lax.psum_scatter(
        jnp.dot(normed, w_out, preferred_element_type=jnp.float32).astype(jnp.bfloat16),
        "head",
        scatter_dimension=0,
        tiled=True,
    )
    return result


def solution(mesh):
    torus = Mesh(mesh.devices.reshape(4, 8, mesh.shape["head"]), ("seq_0", "seq_1", "head"))
    placed = (
        P(SEQ_HEAD, None),
        P(None, "head"),
        P(None, "head"),
        P(),
        P(None, "head"),
        P(None, "head"),
        P(),
        P("head"),
        P("head"),
        P("head"),
        P("head"),
        P("head", None),
    )
    return jax.shard_map(
        per_device, mesh=torus, in_specs=placed, out_specs=P(SEQ_HEAD, None), check_vma=False
    )
```

profile of v0, /device:TPU:8, one launch (start us, length us, event | category | flops | bytes accessed | tf_op | source)
XLA Modules:
  0.0 303.0 jit_solution(5351362348094303624)
XLA Ops:
  9.0 37.6 %all-gather.7.cloned.1.call-done = bf16[1024,2048]{1,0:T(8,128)(2,1)} async-done(((bf16[128,2048]{1,0:T(8,128)(2,1)}), bf16[1024,2048]{1,0:T(8,128)(2,1)}) %all-gather.7.cloned.1.call-update) | async-done | bytes 4194320 | tf_op jit(solution)/shard_map/all_gather | solution.py:100
  46.7 3.9 %fusion.150 = f32[1024,256]{1,0:T(8,128)S(1)} fusion(bf16[1024,2048]{1,0:T(8,128)(2,1)} %all-gather.7.cloned.1.call-done, bf16[2048,256]{1,0:T(8,128)(2,1)} %param.17), kind=kOutput, calls=%fused_computation.216 | convolution fusion | flops 1073741824 | bytes 6291456 | tf_op jit(solution)/shard_map/dot_general | solution.py:105
  50.6 3.6 %collective-permute-start.1 = (f32[3,256]{1,0:T(4,128)S(1)}, f32[3,256]{1,0:T(4,128)S(1)}, u32[]{:S(2)}, u32[]{:S(2)}) collective-permute-start(f32[3,256]{1,0:T(4,128)S(1)} %slice.215), channel_id=1, source_target_pairs={{0,8},{8,16},{16,24},{24,32},{32,40},{40,48},{48,56},{56,64},{64,7... | collective-permute-start | bytes 9224 | tf_op jit(solution)/shard_map/ppermute | solution.py:18
  56.6 3.5 %collective-permute-start = (f32[3,512]{1,0:T(4,128)S(1)}, f32[3,512]{1,0:T(4,128)S(1)}, u32[]{:S(2)}, u32[]{:S(2)}) collective-permute-start(f32[3,512]{1,0:T(4,128)S(1)} %slice.210), channel_id=1, source_target_pairs={{0,8},{8,16},{16,24},{24,32},{32,40},{40,48},{48,56},{56,64},{64,7... | collective-permute-start | bytes 18440 | tf_op jit(solution)/shard_map/ppermute | solution.py:18
  66.5 4.4 %reshape.345 = f32[4,256,8,64]{3,2,1,0:T(8,128)} reshape(f32[1024,512]{1,0:T(8,128)} %divide_multiply_fusion) | data formatting | bytes 4194304 | tf_op jit(solution)/shard_map/reshape | solution.py:143
  70.9 3.8 %copy.48 = f32[4,256,8,64]{1,3,2,0:T(8,128)} copy(f32[4,256,8,64]{3,2,1,0:T(8,128)} %reshape.345) | data formatting | bytes 4194304
  74.7 81.7 %while.17 = (s32[]{:T(128)}, f32[8,64,128]{2,1,0:T(8,128)S(1)}, f32[8]{0:T(128)S(1)}, f32[4,256,8,64]{1,0,3,2:T(4,128)}, f32[4,256,8]{1,2,0:T(8,128)S(1)}, /*ind...) while((s32[]{:T(128)}, f32[8,64,128]{2,1,0:T(8,128)S(1)}, ...), condition=%wide.region_3.4_spmd.clone, body=%wide.region_0.3_spmd.clone.sunk | while | flops 909056064 | bytes 16289238 | solution.py:139
  77.5 3.5 %fusion.182 = f32[256,8,64]{0,2,1:T(8,128)S(1)} fusion(f32[256,256]{1,0:T(8,128)S(1)} %fusion.181, f32[8,256]{1,0:T(8,128)S(1)} %add_bitcast_fusion.4, pred[256,256]{1,0:T(8,128)(4,1)S(1)} %iota_compare_fusion.2, f32[4,256,8,64]{1,3,2,0:T(8,128)} %get-tuple-element.315, s32[]{:T(128)S(6)} %copy.71, f32[256,8]{0,1:T(8,128)S(1)} %dynamic-slice_bitcast_fusion.7), kind=kOutput, calls=%fused_computation.5.clone.1 | convolution fusion | flops 404357120 | bytes 1400836 | tf_op jit(solution)/shard_map/while/body/eval_jaxpr/hts,shp->thp/dot_general | solution.py:62
  82.9 12.3 %dynamic_update_slice.14 = f32[4,256,8,64]{1,0,3,2:T(4,128)} dynamic-update-slice(f32[4,256,8,64]{1,0,3,2:T(4,128)} %get-tuple-element.299, f32[1,256,8,64]{1,0,3,2:T(1,128)S(1)} %copy.63, s32[]{:T(128)S(6)} %copy.71, s32[]{:T(128)} %constant.25.clone.1..sunk, s32[]{:T(128)} %constant.25.clone.1..sunk, s32[]{:T(128)} %constant.25.clone.1..sunk) | dynamic-update-slice | bytes 1048580 | tf_op jit(solution)/shard_map/while/body/jit(dynamic_update_index_in_dim)/dynamic_update_slice | solution.py:139
  97.9 3.5 %fusion.182 = f32[256,8,64]{0,2,1:T(8,128)S(1)} fusion(f32[256,256]{1,0:T(8,128)S(1)} %fusion.181, f32[8,256]{1,0:T(8,128)S(1)} %add_bitcast_fusion.4, pred[256,256]{1,0:T(8,128)(4,1)S(1)} %iota_compare_fusion.2, f32[4,256,8,64]{1,3,2,0:T(8,128)} %get-tuple-element.315, s32[]{:T(128)S(6)} %copy.71, f32[256,8]{0,1:T(8,128)S(1)} %dynamic-slice_bitcast_fusion.7), kind=kOutput, calls=%fused_computation.5.clone.1 | convolution fusion | flops 404357120 | bytes 1400836 | tf_op jit(solution)/shard_map/while/body/eval_jaxpr/hts,shp->thp/dot_general | solution.py:62
  103.3 12.3 %dynamic_update_slice.14 = f32[4,256,8,64]{1,0,3,2:T(4,128)} dynamic-update-slice(f32[4,256,8,64]{1,0,3,2:T(4,128)} %get-tuple-element.299, f32[1,256,8,64]{1,0,3,2:T(1,128)S(1)} %copy.63, s32[]{:T(128)S(6)} %copy.71, s32[]{:T(128)} %constant.25.clone.1..sunk, s32[]{:T(128)} %constant.25.clone.1..sunk, s32[]{:T(128)} %constant.25.clone.1..sunk) | dynamic-update-slice | bytes 1048580 | tf_op jit(solution)/shard_map/while/body/jit(dynamic_update_index_in_dim)/dynamic_update_slice | solution.py:139
  118.4 3.5 %fusion.182 = f32[256,8,64]{0,2,1:T(8,128)S(1)} fusion(f32[256,256]{1,0:T(8,128)S(1)} %fusion.181, f32[8,256]{1,0:T(8,128)S(1)} %add_bitcast_fusion.4, pred[256,256]{1,0:T(8,128)(4,1)S(1)} %iota_compare_fusion.2, f32[4,256,8,64]{1,3,2,0:T(8,128)} %get-tuple-element.315, s32[]{:T(128)S(6)} %copy.71, f32[256,8]{0,1:T(8,128)S(1)} %dynamic-slice_bitcast_fusion.7), kind=kOutput, calls=%fused_computation.5.clone.1 | convolution fusion | flops 404357120 | bytes 1400836 | tf_op jit(solution)/shard_map/while/body/eval_jaxpr/hts,shp->thp/dot_general | solution.py:62
  123.7 12.3 %dynamic_update_slice.14 = f32[4,256,8,64]{1,0,3,2:T(4,128)} dynamic-update-slice(f32[4,256,8,64]{1,0,3,2:T(4,128)} %get-tuple-element.299, f32[1,256,8,64]{1,0,3,2:T(1,128)S(1)} %copy.63, s32[]{:T(128)S(6)} %copy.71, s32[]{:T(128)} %constant.25.clone.1..sunk, s32[]{:T(128)} %constant.25.clone.1..sunk, s32[]{:T(128)} %constant.25.clone.1..sunk) | dynamic-update-slice | bytes 1048580 | tf_op jit(solution)/shard_map/while/body/jit(dynamic_update_index_in_dim)/dynamic_update_slice | solution.py:139
  138.8 3.5 %fusion.182 = f32[256,8,64]{0,2,1:T(8,128)S(1)} fusion(f32[256,256]{1,0:T(8,128)S(1)} %fusion.181, f32[8,256]{1,0:T(8,128)S(1)} %add_bitcast_fusion.4, pred[256,256]{1,0:T(8,128)(4,1)S(1)} %iota_compare_fusion.2, f32[4,256,8,64]{1,3,2,0:T(8,128)} %get-tuple-element.315, s32[]{:T(128)S(6)} %copy.71, f32[256,8]{0,1:T(8,128)S(1)} %dynamic-slice_bitcast_fusion.7), kind=kOutput, calls=%fused_computation.5.clone.1 | convolution fusion | flops 404357120 | bytes 1400836 | tf_op jit(solution)/shard_map/while/body/eval_jaxpr/hts,shp->thp/dot_general | solution.py:62
  144.1 12.3 %dynamic_update_slice.14 = f32[4,256,8,64]{1,0,3,2:T(4,128)} dynamic-update-slice(f32[4,256,8,64]{1,0,3,2:T(4,128)} %get-tuple-element.299, f32[1,256,8,64]{1,0,3,2:T(1,128)S(1)} %copy.63, s32[]{:T(128)S(6)} %copy.71, s32[]{:T(128)} %constant.25.clone.1..sunk, s32[]{:T(128)} %constant.25.clone.1..sunk, s32[]{:T(128)} %constant.25.clone.1..sunk) | dynamic-update-slice | bytes 1048580 | tf_op jit(solution)/shard_map/while/body/jit(dynamic_update_index_in_dim)/dynamic_update_slice | solution.py:139
  158.8 15.8 %all-reduce = f32[64]{0:T(128)S(1)} all-reduce(f32[64]{0:T(128)S(1)} %dynamic-update-slice), channel_id=2, replica_groups=mesh['seq_0'=4,'seq_1'=8,'head'=8] {'seq_1'}, use_global_device_ids=true, to_apply=%add | all-reduce | flops 64 | bytes 512
  174.7 21.7 %all-gather.11.cloned.1.call-done = f32[64,64,128]{2,1,0:T(8,128)} async-done(((f32[8,64,128]{2,1,0:T(8,128)}), f32[64,64,128]{2,1,0:T(8,128)}) %all-gather.11.cloned.1.call-update) | async-done | bytes 2097168 | tf_op jit(solution)/shard_map/all_gather | solution.py:32
  198.9 7.8 %all-gather.2 = f32[4,1,8]{2,1,0:T(1,128)S(1)} all-gather(f32[1,1,8]{2,1,0:T(1,128)S(1)} %get-tuple-element.197), channel_id=1, replica_groups=mesh['seq_0'=4,'seq_1'=8,'head'=8] {'seq_0'}, dimensions={0}, use_global_device_ids=true | all-gather | bytes 160 | tf_op jit(solution)/shard_map/all_gather | solution.py:32
  210.0 13.0 %all-gather.9.cloned.1.call-done = f32[4,8,64,128]{3,2,1,0:T(8,128)} async-done(((f32[1,8,64,128]{3,2,1,0:T(8,128)}), f32[4,8,64,128]{3,2,1,0:T(8,128)}) %all-gather.9.cloned.1.call-update) | async-done | bytes 1048592 | tf_op jit(solution)/shard_map/all_gather | solution.py:32
  223.1 6.3 %multiply_add_fusion = f32[1024,8,64]{0,2,1:T(8,128)} fusion(f32[1024,8,64]{0,2,1:T(8,128)} %reshape.235, f32[1024,8]{0,1:T(8,128)S(1)} %bitcast.186, f32[1024,256]{1,0:T(8,128)} %divide_multiply_fusion.1, f32[4,8,64,128]{3,2,1,0:T(8,128)} %all-gather.9.cloned.1.call-done, f32[64,64,128]{2,1,0:T(8,128)} %all-gather.11.cloned.1.call-done, ...), kind=kOutput, calls=%fused_computation.64 | convolution fusion | flops 808714240 | bytes 7897516 | tf_op jit(solution)/shard_map/tn,hpn->thp/dot_general | solution.py:158
  232.2 7.4 %multiply_reduce_fusion = (f32[1024]{0:T(1024)S(1)}, f32[1024,512]{1,0:T(8,128)}) fusion(f32[1024,512]{1,0:T(8,128)} %copy.52, bf16[1024,2048]{1,0:T(8,128)(2,1)} %all-gather.7.cloned.1.call-done, bf16[2048,512]{1,0:T(8,128)(2,1)} %param.16), kind=kOutput, calls=%fused_computation.62 | convolution fusion | flops 2151152640 | bytes 10489856 | tf_op jit(solution)/shard_map/dot_general | solution.py:104
  239.6 9.5 %all_to_all.6 = f32[8,1,1024]{2,1,0:T(1,128)S(1)} all-to-all(f32[8,1,1024]{2,1,0:T(1,128)S(1)} %broadcast_in_dim.43), channel_id=1, replica_groups=mesh['seq_0'=4,'seq_1'=8,'head'=8] {'head'}, dimensions={0} | all-to-all | bytes 65536 | tf_op jit(solution)/shard_map/all_to_all | solution.py:44
  249.2 6.9 %convolution_convert_fusion = bf16[1024,2048]{1,0:T(8,128)(2,1)} fusion(bf16[512,2048]{1,0:T(8,128)(2,1)S(1)} %copy-done, f32[512]{0:T(512)S(1)} %copy-done.9, f32[1024]{0:T(1024)S(1)} %add_rsqrt_fusion, f32[1024,512]{1,0:T(8,128)} %copy.52, f32[1024,512]{1,0:T(8,128)} %get-tuple-element.209), kind=kOutput, calls=%fused_computation.49 | convolution fusion | flops 2153775104 | bytes 10491904 | tf_op jit(solution)/shard_map/dot_general | solution.py:166
  256.1 40.4 %reduce-scatter.2.cloned.1.call-done = bf16[128,2048]{1,0:T(8,128)(2,1)} async-done(((bf16[1024,2048]{1,0:T(8,128)(2,1)}), bf16[128,2048]{1,0:T(8,128)(2,1)}) %reduce-scatter.2.cloned.1.call-update) | async-done | bytes 524304 | tf_op jit(solution)/shard_map/reduce_scatter | solution.py:165
  (135 shorter events, 40.1 us)
Async XLA Ops:
  6.5 242.6 %copy-start = (bf16[512,2048]{1,0:T(8,128)(2,1)S(1)}, bf16[512,2048]{1,0:T(8,128)(2,1)}, u32[]{:S(2)}) copy-start(bf16[512,2048]{1,0:T(8,128)(2,1)} %param.25) | copy-start | bytes 6291460
  6.5 40.1 %all-gather.7.cloned.1.call-start = ((), (), s32[]{:S(2)}) async-start(), calls=%async_computation.2 | async-start | bytes 4718592 | tf_op jit(solution)/shard_map/all_gather | solution.py:100
  7.3 189.1 %all-gather.11.cloned.1.call-start = ((), (), s32[]{:S(2)}) async-start(), calls=%async_computation.5 | async-start | bytes 2359296 | tf_op jit(solution)/shard_map/all_gather | solution.py:32
  46.7 7.5 %copy-start.3 = (bf16[1024,2048]{1,0:T(8,128)(2,1)S(1)}, bf16[1024,2048]{1,0:T(8,128)(2,1)}, u32[]{:S(2)}) copy-start(bf16[1024,2048]{1,0:T(8,128)(2,1)} %all-gather.7.cloned.1.call-done) | copy-start | bytes 12582916
  46.7 7.6 %copy-start.8 = (bf16[2048,512]{1,0:T(8,128)(2,1)S(1)}, bf16[2048,512]{1,0:T(8,128)(2,1)}, u32[]{:S(2)}) copy-start(bf16[2048,512]{1,0:T(8,128)(2,1)} %param.15) | copy-start | bytes 6291460
  50.6 9.5 %copy-start.4 = (bf16[2048,8]{0,1:T(8,128)(2,1)S(1)}, bf16[2048,8]{0,1:T(8,128)(2,1)}, u32[]{:S(2)}) copy-start(bf16[2048,8]{0,1:T(8,128)(2,1)} %param.18) | copy-start | bytes 98308
  50.6 9.5 %copy-start.6 = (f32[8]{0:T(128)S(1)}, f32[8]{0:T(128)}, u32[]{:S(2)}) copy-start(f32[8]{0:T(128)} %param.22) | copy-start | bytes 100
  50.6 9.5 %copy-start.7 = (f32[8]{0:T(128)S(1)}, f32[8]{0:T(128)}, u32[]{:S(2)}) copy-start(f32[8]{0:T(128)} %param.21) | copy-start | bytes 100
  50.6 10.7 %collective-permute-start.1 = (f32[3,256]{1,0:T(4,128)S(1)}, f32[3,256]{1,0:T(4,128)S(1)}, u32[]{:S(2)}, u32[]{:S(2)}) collective-permute-start(f32[3,256]{1,0:T(4,128)S(1)} %slice.215), channel_id=1, source_target_pairs={{0,8},{8,16},{16,24},{24,32},{32,40},{40,48},{48,56},{56,64},{64,7... | collective-permute-start | bytes 9224 | tf_op jit(solution)/shard_map/ppermute | solution.py:18
  56.6 7.7 %collective-permute-start = (f32[3,512]{1,0:T(4,128)S(1)}, f32[3,512]{1,0:T(4,128)S(1)}, u32[]{:S(2)}, u32[]{:S(2)}) collective-permute-start(f32[3,512]{1,0:T(4,128)S(1)} %slice.210), channel_id=1, source_target_pairs={{0,8},{8,16},{16,24},{24,32},{32,40},{40,48},{48,56},{56,64},{64,7... | collective-permute-start | bytes 18440 | tf_op jit(solution)/shard_map/ppermute | solution.py:18
  70.9 3.8 %copy-start.5 = (f32[8]{0:T(128)S(1)}, f32[8]{0:T(128)}, u32[]{:S(2)}) copy-start(f32[8]{0:T(128)} %param.23) | copy-start | bytes 100
  74.7 82.5 %copy-start.10 = (u32[256]{0:T(256)S(1)}, u32[256]{0:T(256)}, u32[]{:S(2)}) copy-start(u32[256]{0:T(256)} %constant.70) | copy-start | bytes 3076
  76.0 5.0 %copy-start.2 = (f32[4,256,8,64]{1,3,2,0:T(8,128)S(1)}, f32[4,256,8,64]{1,3,2,0:T(8,128)}, u32[]{:S(2)}) copy-start(f32[4,256,8,64]{1,3,2,0:T(8,128)} %get-tuple-element.315) | copy-start | bytes 6291460 | tf_op jit(solution)/shard_map/while
  96.4 5.0 %copy-start.2 = (f32[4,256,8,64]{1,3,2,0:T(8,128)S(1)}, f32[4,256,8,64]{1,3,2,0:T(8,128)}, u32[]{:S(2)}) copy-start(f32[4,256,8,64]{1,3,2,0:T(8,128)} %get-tuple-element.315) | copy-start | bytes 6291460 | tf_op jit(solution)/shard_map/while
  116.8 5.0 %copy-start.2 = (f32[4,256,8,64]{1,3,2,0:T(8,128)S(1)}, f32[4,256,8,64]{1,3,2,0:T(8,128)}, u32[]{:S(2)}) copy-start(f32[4,256,8,64]{1,3,2,0:T(8,128)} %get-tuple-element.315) | copy-start | bytes 6291460 | tf_op jit(solution)/shard_map/while
  137.3 5.0 %copy-start.2 = (f32[4,256,8,64]{1,3,2,0:T(8,128)S(1)}, f32[4,256,8,64]{1,3,2,0:T(8,128)}, u32[]{:S(2)}) copy-start(f32[4,256,8,64]{1,3,2,0:T(8,128)} %get-tuple-element.315) | copy-start | bytes 6291460 | tf_op jit(solution)/shard_map/while
  156.4 0.7 copy-start.1
  157.1 65.9 %all-gather.9.cloned.1.call-start = ((), (), s32[]{:S(2)}) async-start(), calls=%async_computation.3 | async-start | bytes 1310720 | tf_op jit(solution)/shard_map/all_gather | solution.py:32
  198.8 97.6 %reduce-scatter.2.cloned.1.call-start = ((), (), s32[]{:S(2)}) async-start(), calls=%async_computation.4 | async-start | bytes 4718592 | tf_op jit(solution)/shard_map/reduce_scatter | solution.py:165
  232.2 17.0 %copy-start.9 = (f32[512]{0:T(512)S(1)}, f32[512]{0:T(512)}, u32[]{:S(2)}) copy-start(f32[512]{0:T(512)} %param.24) | copy-start | bytes 6148
Sparse Core Ops, SparseCore 0:
  9.2 37.4 all-gather.6
  157.3 39.0 all-gather.10
  199.0 24.0 all-gather.8
  256.2 40.2 reduce-scatter.1
where the time goes:
time: 305 us; the launch traced here: 303 us
  waiting for transfers between devices  115 us (38%)
  local copies, waits for them, and re-layouts  75.1 us (25%)
  matrix products  48.5 us (16%)
  blocking collectives  33.1 us (11%)
  between operations  14 us (5%)
  other arithmetic  10.2 us (3%)
  starting transfers between devices  7.17 us (2%)
    dynamic_update_slice x8, local copies, waits for them, and re-layouts, per_device(): lax.scan(advance, (empty_state, empty_decay), (x_conv.reshape(spans, SPAN...  51.4 us
    reduce_scatter x1, waiting for transfers between devices, per_device(): lax.psum_scatter(jnp.dot(normed, w_out, preferred_element_type=jnp.float3...  40.4 us
    all_gather x1, waiting for transfers between devices, per_device(): block_rows = lax.all_gather(tokens, 'head', axis=0, tiled=True)  37.6 us
    all_gather x2, waiting for transfers between devices, entering_2(): pieces = jax.tree.map(lambda part: lax.all_gather(part, axis), running)  34.7 us
    unnamed x1, blocking collectives  15.8 us
    dot_general x4, matrix products, span_update(): jnp.einsum('hts,shp->thp', within * scores[None], scaled, precision=highest)  13.9 us
    all_to_all x1, blocking collectives, sent_to_all(): lax.all_to_all(jnp.broadcast_to(shard[None], (size, *shard.shape)), axis,...  9.5 us
    all_gather x1, blocking collectives, entering_2(): pieces = jax.tree.map(lambda part: lax.all_gather(part, axis), running)  7.78 us
  transfers between devices with their start and end apart: 6, of which 5 were waited for; matrix products, arithmetic and copies ran while one was open for 4% of the time, Pallas kernels for 0%

commit v1 on v0

--- a/solution.py
+++ b/solution.py
@@ -97,7 +97,10 @@
     head_count = dt_bias.shape[0]
     head_width = inner_cols // head_count
     state_size = w_in_bc.shape[1] // 2
-    block_rows = lax.all_gather(tokens, "head", axis=0, tiled=True)
+    n_dev = lax.axis_size("head")
+    blocks = jnp.stack([tokens for _ in range(n_dev)])
+    blocks = lax.all_to_all(blocks, "head", split_axis=0, concat_axis=0)
+    block_rows = jnp.concatenate(blocks, axis=0)
     joined = jnp.concatenate(
         [
             jnp.dot(block_rows, w_in_x, preferred_element_type=jnp.float32),

time: 305 us -> 336 us (1.10)
  matrix products: 48.5 us -> 61 us
  waiting for transfers between devices: 115 us -> 124 us
  starting transfers between devices: 7.17 us -> 12.8 us
    all_to_all x0 -> x1, waiting for transfers between devices: none -> 49.5 us  [per_device(): blocks = lax.all_to_all(blocks, 'head', split_axis=0, concat_axis=0)]
    all_gather x1 -> x0, waiting for transfers between devices: 37.6 us -> none  [per_device(): block_rows = lax.all_gather(tokens, 'head', axis=0, tiled=True)]
    all_to_all x0 -> x1, starting transfers between devices: none -> 4.69 us  [per_device(): blocks = lax.all_to_all(blocks, 'head', split_axis=0, concat_axis=0)]
    dot_general x4, matrix products: 2.36 us -> 6.56 us  [span_update(): jnp.einsum('tn,hpn->thp', c_span, state, precision=highest)]
    dot_general x4, matrix products: 2.72 us -> 6.88 us  [span_update(): jnp.einsum('shp,sn->hpn', scaled * remain[:, :, None], b_span, precision=...]
    another operation x4 -> x5, local copies, waits for them, and re-layouts: 0.02 us -> 3.7 us  [the longest x1 3.68 us: per_device(): blocks = jnp.stack([tokens for _ in range(n_dev)])]
  transfers between devices with their start and end apart: 6 -> 6, of which waited for: 5 -> 4; matrix products, arithmetic and copies ran while one was open for 4% -> 4% of each run, Pallas kernels for 0% -> 0%
where the time goes in v1:
time: 336 us; the launch traced here: 333 us
  waiting for transfers between devices  124 us (37%)
  local copies, waits for them, and re-layouts  76.6 us (23%)
  matrix products  61 us (18%)
  blocking collectives  34.4 us (10%)
  between operations  14.1 us (4%)
  starting transfers between devices  12.8 us (4%)
  other arithmetic  10.2 us (3%)
    dynamic_update_slice x8, local copies, waits for them, and re-layouts, per_device(): lax.scan(advance, (empty_state, empty_decay), (x_conv.reshape(spans, SPAN...  51.4 us
    all_to_all x1, waiting for transfers between devices, per_device(): blocks = lax.all_to_all(blocks, 'head', split_axis=0, concat_axis=0)  49.5 us
    reduce_scatter x1, waiting for transfers between devices, per_device(): lax.psum_scatter(jnp.dot(normed, w_out, preferred_element_type=jnp.float3...  40.4 us
    all_gather x2, waiting for transfers between devices, entering_2(): pieces = jax.tree.map(lambda part: lax.all_gather(part, axis), running)  34.1 us
    unnamed x1, blocking collectives  17.1 us
    dot_general x4, matrix products, span_update(): jnp.einsum('hts,shp->thp', within * scores[None], scaled, precision=highest)  13.9 us
    all_to_all x1, blocking collectives, sent_to_all(): lax.all_to_all(jnp.broadcast_to(shard[None], (size, *shard.shape)), axis,...  9.5 us
    all_gather x1, blocking collectives, entering_2(): pieces = jax.tree.map(lambda part: lax.all_gather(part, axis), running)  7.85 us
  transfers between devices with their start and end apart: 6, of which 4 were waited for; matrix products, arithmetic and copies ran while one was open for 4% of the time, Pallas kernels for 0%

profile of v1, /device:TPU:8, one launch (start us, length us, event | category | flops | bytes accessed | tf_op | source)
XLA Modules:
  0.0 333.5 jit_solution(8444597655974495141)
XLA Ops:
  6.5 3.7 %stack.2 = bf16[8,128,2048]{2,1,0:T(8,128)(2,1)} broadcast(bf16[128,2048]{1,0:T(8,128)(2,1)} %param.14), dimensions={1,2} | broadcast | bytes 4718592 | tf_op jit(solution)/shard_map/stack | solution.py:101
  10.2 4.7 %all-to-all-start = ((bf16[8,128,2048]{2,1,0:T(8,128)(2,1)}), bf16[8,128,2048]{2,1,0:T(8,128)(2,1)}, u32[]{:S(2)}, u32[]{:S(2)}) async-start(bf16[8,128,2048]{2,1,0:T(8,128)(2,1)} %stack.2), calls=%async_computation | async-start | bytes 8388608 | tf_op jit(solution)/shard_map/all_to_all | solution.py:102
  15.1 49.5 %all-to-all-done = bf16[8,128,2048]{2,1,0:T(8,128)(2,1)} async-done(((bf16[8,128,2048]{2,1,0:T(8,128)(2,1)}), bf16[8,128,2048]{2,1,0:T(8,128)(2,1)}, u32[]{:S(2)}, u32[]{:S(2)}) %all-to-all-start) | async-done | bytes 4194336 | tf_op jit(solution)/shard_map/all_to_all | solution.py:102
  64.6 3.9 %fusion.150 = f32[1024,256]{1,0:T(8,128)S(1)} fusion(bf16[1024,2048]{1,0:T(8,128)(2,1)} %bitcast, bf16[2048,256]{1,0:T(8,128)(2,1)} %param.17), kind=kOutput, calls=%fused_computation.216 | convolution fusion | flops 1073741824 | bytes 6291456 | tf_op jit(solution)/shard_map/dot_general | solution.py:108
  68.5 4.0 %collective-permute-start.1 = (f32[3,256]{1,0:T(4,128)S(1)}, f32[3,256]{1,0:T(4,128)S(1)}, u32[]{:S(2)}, u32[]{:S(2)}) collective-permute-start(f32[3,256]{1,0:T(4,128)S(1)} %slice.215), channel_id=1, source_target_pairs={{0,8},{8,16},{16,24},{24,32},{32,40},{40,48},{48,56},{56,64},{64,7... | collective-permute-start | bytes 9224 | tf_op jit(solution)/shard_map/ppermute | solution.py:18
  72.5 4.5 %fusion.149 = f32[1024,512]{1,0:T(8,128)S(1)} fusion(bf16[1024,2048]{1,0:T(8,128)(2,1)} %bitcast, bf16[2048,512]{1,0:T(8,128)(2,1)S(1)} %copy-done.9), kind=kOutput, calls=%fused_computation.215 | convolution fusion | flops 2147483648 | bytes 8388608 | tf_op jit(solution)/shard_map/dot_general | solution.py:106
  77.0 3.8 %collective-permute-start = (f32[3,512]{1,0:T(4,128)S(1)}, f32[3,512]{1,0:T(4,128)S(1)}, u32[]{:S(2)}, u32[]{:S(2)}) collective-permute-start(f32[3,512]{1,0:T(4,128)S(1)} %slice.210), channel_id=1, source_target_pairs={{0,8},{8,16},{16,24},{24,32},{32,40},{40,48},{48,56},{56,64},{64,7... | collective-permute-start | bytes 18440 | tf_op jit(solution)/shard_map/ppermute | solution.py:18
  88.2 4.4 %reshape.351 = f32[4,256,8,64]{3,2,1,0:T(8,128)} reshape(f32[1024,512]{1,0:T(8,128)} %divide_multiply_fusion) | data formatting | bytes 4194304 | tf_op jit(solution)/shard_map/reshape | solution.py:146
  92.7 3.8 %copy.48 = f32[4,256,8,64]{1,3,2,0:T(8,128)} copy(f32[4,256,8,64]{3,2,1,0:T(8,128)} %reshape.351) | data formatting | bytes 4194304
  96.5 89.5 %while.17 = (s32[]{:T(128)}, f32[8,64,128]{2,1,0:T(8,128)S(1)}, f32[8]{0:T(128)S(1)}, f32[4,256,8,64]{1,0,3,2:T(4,128)}, f32[4,256,8]{1,2,0:T(8,128)S(1)}, /*ind...) while((s32[]{:T(128)}, f32[8,64,128]{2,1,0:T(8,128)S(1)}, ...), condition=%wide.region_3.4_spmd.clone, body=%wide.region_0.3_spmd.clone.sunk | while | flops 909056064 | bytes 7901610 | solution.py:142
  98.7 3.5 %fusion.182 = f32[256,8,64]{0,2,1:T(8,128)S(1)} fusion(f32[256,256]{1,0:T(8,128)S(1)} %fusion.181, f32[8,256]{1,0:T(8,128)S(1)} %add_bitcast_fusion.4, pred[256,256]{1,0:T(8,128)(4,1)S(1)} %iota_compare_fusion.2, f32[4,256,8,64]{1,3,2,0:T(8,128)} %get-tuple-element.315, s32[]{:T(128)} %get-tuple-element.296, f32[256,8]{0,1:T(8,128)S(1)} %dynamic-slice_bitcast_fusion.7), kind=kOutput, calls=%fused_computation.5.clone.1 | convolution fusion | flops 404357120 | bytes 1401344 | tf_op jit(solution)/shard_map/while/body/eval_jaxpr/hts,shp->thp/dot_general | solution.py:62
  104.8 12.3 %dynamic_update_slice.14 = f32[4,256,8,64]{1,0,3,2:T(4,128)} dynamic-update-slice(f32[4,256,8,64]{1,0,3,2:T(4,128)} %get-tuple-element.299, f32[1,256,8,64]{1,0,3,2:T(1,128)S(1)} %copy.63, s32[]{:T(128)} %get-tuple-element.296, s32[]{:T(128)} %constant.25.clone.1..sunk, s32[]{:T(128)} %constant.25.clone.1..sunk, s32[]{:T(128)} %constant.25.clone.1..sunk) | dynamic-update-slice | bytes 1048580 | tf_op jit(solution)/shard_map/while/body/jit(dynamic_update_index_in_dim)/dynamic_update_slice | solution.py:142
  127.1 12.3 %dynamic_update_slice.14 = f32[4,256,8,64]{1,0,3,2:T(4,128)} dynamic-update-slice(f32[4,256,8,64]{1,0,3,2:T(4,128)} %get-tuple-element.299, f32[1,256,8,64]{1,0,3,2:T(1,128)S(1)} %copy.63, s32[]{:T(128)} %get-tuple-element.296, s32[]{:T(128)} %constant.25.clone.1..sunk, s32[]{:T(128)} %constant.25.clone.1..sunk, s32[]{:T(128)} %constant.25.clone.1..sunk) | dynamic-update-slice | bytes 1048580 | tf_op jit(solution)/shard_map/while/body/jit(dynamic_update_index_in_dim)/dynamic_update_slice | solution.py:142
  149.5 12.3 %dynamic_update_slice.14 = f32[4,256,8,64]{1,0,3,2:T(4,128)} dynamic-update-slice(f32[4,256,8,64]{1,0,3,2:T(4,128)} %get-tuple-element.299, f32[1,256,8,64]{1,0,3,2:T(1,128)S(1)} %copy.63, s32[]{:T(128)} %get-tuple-element.296, s32[]{:T(128)} %constant.25.clone.1..sunk, s32[]{:T(128)} %constant.25.clone.1..sunk, s32[]{:T(128)} %constant.25.clone.1..sunk) | dynamic-update-slice | bytes 1048580 | tf_op jit(solution)/shard_map/while/body/jit(dynamic_update_index_in_dim)/dynamic_update_slice | solution.py:142
  171.9 12.3 %dynamic_update_slice.14 = f32[4,256,8,64]{1,0,3,2:T(4,128)} dynamic-update-slice(f32[4,256,8,64]{1,0,3,2:T(4,128)} %get-tuple-element.299, f32[1,256,8,64]{1,0,3,2:T(1,128)S(1)} %copy.63, s32[]{:T(128)} %get-tuple-element.296, s32[]{:T(128)} %constant.25.clone.1..sunk, s32[]{:T(128)} %constant.25.clone.1..sunk, s32[]{:T(128)} %constant.25.clone.1..sunk) | dynamic-update-slice | bytes 1048580 | tf_op jit(solution)/shard_map/while/body/jit(dynamic_update_index_in_dim)/dynamic_update_slice | solution.py:142
  188.5 17.1 %all-reduce = f32[64]{0:T(128)S(1)} all-reduce(f32[64]{0:T(128)S(1)} %dynamic-update-slice), channel_id=2, replica_groups=mesh['seq_0'=4,'seq_1'=8,'head'=8] {'seq_1'}, use_global_device_ids=true, to_apply=%add | all-reduce | flops 64 | bytes 512
  205.7 21.2 %all-gather.8.cloned.1.call-done = f32[64,64,128]{2,1,0:T(8,128)} async-done(((f32[8,64,128]{2,1,0:T(8,128)}), f32[64,64,128]{2,1,0:T(8,128)}) %all-gather.8.cloned.1.call-update) | async-done | bytes 2097168 | tf_op jit(solution)/shard_map/all_gather | solution.py:32
  229.4 7.8 %all-gather.2 = f32[4,1,8]{2,1,0:T(1,128)S(1)} all-gather(f32[1,1,8]{2,1,0:T(1,128)S(1)} %get-tuple-element.197), channel_id=1, replica_groups=mesh['seq_0'=4,'seq_1'=8,'head'=8] {'seq_0'}, dimensions={0}, use_global_device_ids=true | all-gather | bytes 160 | tf_op jit(solution)/shard_map/all_gather | solution.py:32
  240.7 12.9 %all-gather.6.cloned.1.call-done = f32[4,8,64,128]{3,2,1,0:T(8,128)} async-done(((f32[1,8,64,128]{3,2,1,0:T(8,128)}), f32[4,8,64,128]{3,2,1,0:T(8,128)}) %all-gather.6.cloned.1.call-update) | async-done | bytes 1048592 | tf_op jit(solution)/shard_map/all_gather | solution.py:32
  253.7 6.1 %multiply_add_fusion = f32[1024,8,64]{0,2,1:T(8,128)} fusion(f32[1024,8,64]{0,2,1:T(8,128)} %reshape.241, f32[1024,8]{0,1:T(8,128)S(1)} %bitcast.189, f32[1024,256]{1,0:T(8,128)S(1)} %bitcast.186, f32[4,8,64,128]{3,2,1,0:T(8,128)} %all-gather.6.cloned.1.call-done, f32[64,64,128]{2,1,0:T(8,128)} %all-gather.8.cloned.1.call-done, ...), kind=kOutput, calls=%fused_computation.64 | convolution fusion | flops 808714240 | bytes 7903756 | tf_op jit(solution)/shard_map/tn,hpn->thp/dot_general | solution.py:161
  262.7 7.4 %multiply_reduce_fusion = (f32[1024]{0:T(1024)S(1)}, f32[1024,512]{1,0:T(8,128)}) fusion(f32[1024,512]{1,0:T(8,128)} %copy.52, bf16[1024,2048]{1,0:T(8,128)(2,1)} %bitcast, bf16[2048,512]{1,0:T(8,128)(2,1)} %param.16), kind=kOutput, calls=%fused_computation.62 | convolution fusion | flops 2151152640 | bytes 10489856 | tf_op jit(solution)/shard_map/dot_general | solution.py:107
  270.1 9.5 %all_to_all.11 = f32[8,1,1024]{2,1,0:T(1,128)S(1)} all-to-all(f32[8,1,1024]{2,1,0:T(1,128)S(1)} %broadcast_in_dim.43), channel_id=1, replica_groups=mesh['seq_0'=4,'seq_1'=8,'head'=8] {'head'}, dimensions={0} | all-to-all | bytes 65536 | tf_op jit(solution)/shard_map/all_to_all | solution.py:44
  279.6 6.9 %convolution_convert_fusion = bf16[1024,2048]{1,0:T(8,128)(2,1)} fusion(bf16[512,2048]{1,0:T(8,128)(2,1)S(1)} %copy-done, f32[512]{0:T(512)S(1)} %copy-done.10, f32[1024]{0:T(1024)S(1)} %add_rsqrt_fusion, f32[1024,512]{1,0:T(8,128)} %copy.52, f32[1024,512]{1,0:T(8,128)} %get-tuple-element.209), kind=kOutput, calls=%fused_computation.49 | convolution fusion | flops 2153775104 | bytes 10491904 | tf_op jit(solution)/shard_map/dot_general | solution.py:169
  286.6 40.4 %reduce-scatter.2.cloned.1.call-done = bf16[128,2048]{1,0:T(8,128)(2,1)} async-done(((bf16[1024,2048]{1,0:T(8,128)(2,1)}), bf16[128,2048]{1,0:T(8,128)(2,1)}) %reduce-scatter.2.cloned.1.call-update) | async-done | bytes 524304 | tf_op jit(solution)/shard_map/reduce_scatter | solution.py:168
  (131 shorter events, 54.8 us)
Async XLA Ops:
  6.5 273.1 %copy-start = (bf16[512,2048]{1,0:T(8,128)(2,1)S(1)}, bf16[512,2048]{1,0:T(8,128)(2,1)}, u32[]{:S(2)}) copy-start(bf16[512,2048]{1,0:T(8,128)(2,1)} %param.25) | copy-start | bytes 6291460
  10.2 4.8 %copy-start.6 = (f32[4,256]{1,0:T(4,128)S(1)}, f32[4,256]{1,0:T(4,128)}, u32[]{:S(2)}) copy-start(f32[4,256]{1,0:T(4,128)} %param.20) | copy-start | bytes 12292
  10.2 4.8 %copy-start.5 = (f32[4,512]{1,0:T(4,128)S(1)}, f32[4,512]{1,0:T(4,128)}, u32[]{:S(2)}) copy-start(f32[4,512]{1,0:T(4,128)} %param.19) | copy-start | bytes 24580
  10.2 54.3 %all-to-all-start = ((bf16[8,128,2048]{2,1,0:T(8,128)(2,1)}), bf16[8,128,2048]{2,1,0:T(8,128)(2,1)}, u32[]{:S(2)}, u32[]{:S(2)}) async-start(bf16[8,128,2048]{2,1,0:T(8,128)(2,1)} %stack.2), calls=%async_computation | async-start | bytes 8388608 | tf_op jit(solution)/shard_map/all_to_all | solution.py:102
  14.9 212.0 %all-gather.8.cloned.1.call-start = ((), (), s32[]{:S(2)}) async-start(), calls=%async_computation.5 | async-start | bytes 2359296 | tf_op jit(solution)/shard_map/all_gather | solution.py:32
  64.6 7.9 %copy-start.9 = (bf16[2048,512]{1,0:T(8,128)(2,1)S(1)}, bf16[2048,512]{1,0:T(8,128)(2,1)}, u32[]{:S(2)}) copy-start(bf16[2048,512]{1,0:T(8,128)(2,1)} %param.15) | copy-start | bytes 6291460
  68.5 12.4 %copy-start.3 = (bf16[2048,8]{0,1:T(8,128)(2,1)S(1)}, bf16[2048,8]{0,1:T(8,128)(2,1)}, u32[]{:S(2)}) copy-start(bf16[2048,8]{0,1:T(8,128)(2,1)} %param.18) | copy-start | bytes 98308
  68.5 12.4 %copy-start.7 = (f32[8]{0:T(128)S(1)}, f32[8]{0:T(128)}, u32[]{:S(2)}) copy-start(f32[8]{0:T(128)} %param.22) | copy-start | bytes 100
  68.5 12.4 %copy-start.8 = (f32[8]{0:T(128)S(1)}, f32[8]{0:T(128)}, u32[]{:S(2)}) copy-start(f32[8]{0:T(128)} %param.21) | copy-start | bytes 100
  68.5 15.8 %collective-permute-start.1 = (f32[3,256]{1,0:T(4,128)S(1)}, f32[3,256]{1,0:T(4,128)S(1)}, u32[]{:S(2)}, u32[]{:S(2)}) collective-permute-start(f32[3,256]{1,0:T(4,128)S(1)} %slice.215), channel_id=1, source_target_pairs={{0,8},{8,16},{16,24},{24,32},{32,40},{40,48},{48,56},{56,64},{64,7... | collective-permute-start | bytes 9224 | tf_op jit(solution)/shard_map/ppermute | solution.py:18
  77.0 9.0 %collective-permute-start = (f32[3,512]{1,0:T(4,128)S(1)}, f32[3,512]{1,0:T(4,128)S(1)}, u32[]{:S(2)}, u32[]{:S(2)}) collective-permute-start(f32[3,512]{1,0:T(4,128)S(1)} %slice.210), channel_id=1, source_target_pairs={{0,8},{8,16},{16,24},{24,32},{32,40},{40,48},{48,56},{56,64},{64,7... | collective-permute-start | bytes 18440 | tf_op jit(solution)/shard_map/ppermute | solution.py:18
  92.7 3.8 %copy-start.4 = (f32[8]{0:T(128)S(1)}, f32[8]{0:T(128)}, u32[]{:S(2)}) copy-start(f32[8]{0:T(128)} %param.23) | copy-start | bytes 100
  96.5 90.5 %copy-start.11 = (u32[256]{0:T(256)S(1)}, u32[256]{0:T(256)}, u32[]{:S(2)}) copy-start(u32[256]{0:T(256)} %constant.70) | copy-start | bytes 3076
  186.0 0.7 copy-start.1
  186.7 67.0 %all-gather.6.cloned.1.call-start = ((), (), s32[]{:S(2)}) async-start(), calls=%async_computation.3 | async-start | bytes 1310720 | tf_op jit(solution)/shard_map/all_gather | solution.py:32
  229.4 97.6 %reduce-scatter.2.cloned.1.call-start = ((), (), s32[]{:S(2)}) async-start(), calls=%async_computation.4 | async-start | bytes 4718592 | tf_op jit(solution)/shard_map/reduce_scatter | solution.py:168
  237.3 16.4 %copy-start.2 = (f32[4,256,256]{2,1,0:T(8,128)S(1)}, f32[4,256,256]{2,1,0:T(8,128)}, u32[]{:S(2)}) copy-start(f32[4,256,256]{2,1,0:T(8,128)} %get-tuple-element.329) | copy-start | bytes 3145732
  262.7 17.0 %copy-start.10 = (f32[512]{0:T(512)S(1)}, f32[512]{0:T(512)}, u32[]{:S(2)}) copy-start(f32[512]{0:T(512)} %param.24) | copy-start | bytes 6148
Sparse Core Ops, SparseCore 0:
  186.8 40.0 all-gather.7
  229.5 24.1 all-gather.5
  286.7 40.2 reduce-scatter.1
